TPU v7x, 256 devices: a whole 4x4x8 slice. The times are simulated.
256 devices in a mesh: freq: 32 (over z, x_lo, core), rcv: 8 (over x_hi, y).
Axes of the slice: x: 4 (x_hi: 2, x_lo: 2; x = x_hi * 2 + x_lo), y: 4, z: 8, core: 2. Of those that a mesh axis runs over, the one named last changes fastest.
Arguments:
- reflection: bfloat16 [2, 128, 768, 768], P(None, 'freq', 'rcv'), may hold values from -0.21875 to 0.21875
- direct: bfloat16 [768, 128, 512], P(('rcv', 'freq')), may hold values from -6 to 6
- onset: int32 [768, 128], P(('rcv', 'freq')), may hold values from 128 to 383
Outputs:
- focus_plus: bfloat16 [768, 128, 512], P(('rcv', 'freq'))
- focus_minus: bfloat16 [768, 128, 512], P(('rcv', 'freq'))
- correlation: float32 [2, 128, 128, 128], P(None, 'freq', 'rcv')
All inputs are finite; a program needn't handle non-finite values.
Results may differ from a plain program's by a relative error of at most 0.019.
Values may be sent and summed in bfloat16 or wider, within the bound.
No kernel may reach another device: no remote copies, remote signals or barrier semaphores. Data moves between devices by JAX's collectives and lax.ppermute only.
A program may use at most 64 MiB of HBM per device.

v0:
```python
import math

import jax
import jax.numpy as jnp
from jax import lax
from jax.sharding import PartitionSpec as P


def cut_along(value, dim, peers):
    before, after = (value.shape[:dim], value.shape[dim + 1 :])
    return jnp.moveaxis(value.reshape(*before, peers, -1, *after), dim, 0)


def sum_at_owner(value, axis, dim):
    parts = cut_along(value, dim, lax.axis_size(axis))
    arrived = lax.all_to_all(parts, axis, split_axis=0, concat_axis=0, tiled=True)
    return arrived.astype(jnp.float32).sum(axis=0)


def lookup_tables(samples, frequencies):
    sample = jnp.arange(samples, dtype=jnp.int32)
    spectral_bin_index = jnp.arange(frequencies, dtype=jnp.int32)
    phase_index = sample[:, None] * spectral_bin_index[None, :] % samples
    angles = 2.0 * math.pi / samples * phase_index.astype(jnp.float32)
    cosine = jnp.cos(angles)
    sine = jnp.sin(angles)
    forward = (jnp.stack([cosine, -sine], axis=1) / math.sqrt(samples)).astype(jnp.bfloat16)
    inverse = (jnp.stack([cosine.T, -sine.T], axis=0) * (2.0 / math.sqrt(samples))).astype(
        jnp.bfloat16
    )
    return (forward, inverse)


def fourier_spectrum(field, forward):
    local_spectra = jnp.einsum(
        "sqt,tcf->scfq", field, forward, preferred_element_type=jnp.float32
    ).astype(jnp.bfloat16)
    return lax.all_to_all(local_spectra, "freq", split_axis=2, concat_axis=0, tiled=True)


def make_term(spectra, reflection, conj_sign):
    spectrum_real_rows = spectra[:, 0]
    spec_imag = spectra[:, 1]

    def product(left_operand, right_operand):
        return jnp.einsum(
            "key,ekn->ykn", left_operand, right_operand, preferred_element_type=jnp.float32
        )

    real_part = product(reflection[0], spectrum_real_rows) - conj_sign * product(
        reflection[1], spec_imag
    )
    imag_part = product(reflection[0], spec_imag) + conj_sign * product(
        reflection[1], spectrum_real_rows
    )
    return jnp.stack([real_part, imag_part], axis=1)


def to_time(spectra, reflection, conj_sign):
    summed = sum_at_owner(make_term(spectra, reflection, conj_sign).astype(jnp.bfloat16), "rcv", 0)
    return lax.all_to_all(
        summed.astype(jnp.bfloat16), "freq", split_axis=0, concat_axis=2, tiled=True
    )


def inverse_window(summed, onset, inverse):
    traces = jnp.einsum("scfq,cft->sqt", summed, inverse, preferred_element_type=jnp.float32)
    sample = jnp.arange(traces.shape[2], dtype=jnp.int32)
    window = (sample[None, None, :] < onset[:, :, None]).astype(jnp.float32)
    return traces * window


def on_device(reflection, direct, onset):
    samples = direct.shape[2]
    frequencies = reflection.shape[1] * lax.axis_size("freq")
    forward, inverse = lookup_tables(samples, frequencies)
    focus_plus = direct
    minus_spectrum = None
    plus_spectrum = fourier_spectrum(focus_plus, forward)
    focus_minus = inverse_window(to_time(plus_spectrum, reflection, 1.0), onset, inverse).astype(
        jnp.bfloat16
    )
    minus_spectrum = fourier_spectrum(focus_minus, forward)
    returned = inverse_window(to_time(minus_spectrum, reflection, -1.0), onset, inverse)
    focus_plus = (direct.astype(jnp.float32) + returned).astype(jnp.bfloat16)
    plus_spectrum = fourier_spectrum(focus_plus, forward)
    receivers = reflection.shape[3]
    summed = sum_at_owner(make_term(plus_spectrum, reflection, 1.0).astype(jnp.bfloat16), "rcv", 0)
    green_field = (summed - minus_spectrum.astype(jnp.float32)).astype(jnp.bfloat16)
    green_real = green_field[:, 0]
    green_imag = green_field[:, 1]

    def pairwise(left_operand, right_operand):
        return jnp.einsum(
            "rfa,rfb->fab", left_operand, right_operand, preferred_element_type=jnp.float32
        )

    real_part = pairwise(green_real, green_real) + pairwise(green_imag, green_imag)
    imag_part = pairwise(green_real, green_imag) - pairwise(green_imag, green_real)
    partial_corr = jnp.stack([real_part, imag_part], axis=0) / receivers
    correlation = sum_at_owner(partial_corr.astype(jnp.bfloat16), "rcv", 2)
    return (focus_plus, focus_minus, correlation)


def solution(mesh):
    placed = (
        P(None, "freq", "rcv", None),
        P(("rcv", "freq"), None, None),
        P(("rcv", "freq"), None),
    )
    return jax.shard_map(
        on_device,
        mesh=mesh,
        in_specs=placed,
        out_specs=(
            P(("rcv", "freq"), None, None),
            P(("rcv", "freq"), None, None),
            P(None, "freq", "rcv", None),
        ),
        check_vma=False,
    )
```

profile of v0, /device:TPU:2, one launch (start us, length us, event | category | flops | bytes accessed | tf_op | source)
XLA Modules:
  0.0 202.6 jit_solution(4122049955311328391)
XLA Ops:
  0.6 1.0 sine_negate_fusion.1
  1.7 1.3 fusion.11
  3.0 0.2 copy.61
  3.2 20.5 %all_to_all.110 = bf16[3,2,128,128]{3,1,0,2:T(2,128)(2,1)S(1)} all-to-all(bf16[3,2,128,128]{3,1,0,2:T(2,128)(2,1)S(1)} %copy.61), channel_id=1, replica_groups=mesh['freq'=32,'rcv'=8] {'freq'}, dimensions={2} | all-to-all | bytes 393216 | tf_op jit(solution)/shard_map/all_to_all | solution.py:38
  23.8 0.1 copy.62
  23.8 0.1 fusion.79
  23.9 0.4 fusion.30
  24.3 0.4 fusion.28
  24.7 1.3 fusion
  26.1 2.3 %copy.65 = bf16[768,4,128]{2,0,1:T(8,128)(2,1)} copy(bf16[768,4,128]{0,2,1:T(8,128)(2,1)} %fusion) | data formatting | bytes 1572864 | tf_op jit(solution)/shard_map/sub | solution.py:50
  28.4 1.3 fusion.1
  29.7 1.6 copy.66
  31.3 0.1 pad_maximum_fusion
  31.4 0.2 copy.67
  31.6 28.0 %all_to_all.111 = bf16[8,96,2,4,128]{4,1,3,2,0:T(8,128)(2,1)S(1)} all-to-all(bf16[8,96,2,4,128]{4,1,3,2,0:T(8,128)(2,1)S(1)} %copy.67), channel_id=1, replica_groups=mesh['freq'=32,'rcv'=8] {'rcv'}, dimensions={0} | all-to-all | bytes 3145728 | tf_op jit(solution)/shard_map/all_to_all | solution.py:16
  59.6 0.2 reduce_sum.42
  59.9 0.8 copy.69
  60.6 5.0 %all-to-all-start.2 = ((bf16[96,2,4,128]{3,2,1,0:T(4,128)(2,1)}), bf16[96,2,4,128]{3,2,1,0:T(4,128)(2,1)S(1)}, u32[]{:S(2)}, u32[]{:S(2)}) async-start(bf16[96,2,4,128]{3,2,1,0:T(4,128)(2,1)} %copy.69), calls=%async_computation.2 | async-start | bytes 393216 | tf_op jit(solution)/shard_map/all_to_all | solution.py:61
  65.7 1.0 sine_negate_fusion
  66.7 9.7 %all-to-all-done.2 = bf16[96,2,4,128]{3,2,1,0:T(4,128)(2,1)S(1)} async-done(((bf16[96,2,4,128]{3,2,1,0:T(4,128)(2,1)}), bf16[96,2,4,128]{3,2,1,0:T(4,128)(2,1)S(1)}, u32[]{:S(2)}, u32[]{:S(2)}) %all-to-all-start.2) | async-done | bytes 196640 | tf_op jit(solution)/shard_map/all_to_all | solution.py:61
  76.4 0.1 copy.70
  76.5 0.3 fusion.7
  76.8 0.3 fusion.12
  77.1 0.2 copy.72
  77.3 14.0 %all_to_all.112 = bf16[3,2,128,128]{3,1,0,2:T(2,128)(2,1)S(1)} all-to-all(bf16[3,2,128,128]{3,1,0,2:T(2,128)(2,1)S(1)} %copy.72), channel_id=1, replica_groups=mesh['freq'=32,'rcv'=8] {'freq'}, dimensions={2} | all-to-all | bytes 393216 | tf_op jit(solution)/shard_map/all_to_all | solution.py:38
  91.3 0.1 copy.73
  91.5 0.6 copy-done.3
  92.1 0.4 fusion.24
  92.5 0.4 fusion.26
  92.9 1.3 fusion.3
  94.2 2.3 %copy.77 = bf16[768,4,128]{2,0,1:T(8,128)(2,1)} copy(bf16[768,4,128]{0,2,1:T(8,128)(2,1)} %fusion.3) | data formatting | bytes 1572864 | tf_op jit(solution)/shard_map/add | solution.py:53
  96.5 1.3 fusion.2
  97.8 1.6 copy.76
  99.4 0.1 pad_maximum_fusion.1
  99.6 0.2 copy.78
  99.7 24.9 %all_to_all.113 = bf16[8,96,2,4,128]{4,1,3,2,0:T(8,128)(2,1)S(1)} all-to-all(bf16[8,96,2,4,128]{4,1,3,2,0:T(8,128)(2,1)S(1)} %copy.78), channel_id=1, replica_groups=mesh['freq'=32,'rcv'=8] {'rcv'}, dimensions={0} | all-to-all | bytes 3145728 | tf_op jit(solution)/shard_map/all_to_all | solution.py:16
  124.7 0.2 reduce_sum.43
  124.9 0.1 copy.80
  125.0 14.6 %all_to_all.114 = bf16[96,2,4,128]{3,2,1,0:T(4,128)(2,1)S(1)} all-to-all(bf16[96,2,4,128]{3,2,1,0:T(4,128)(2,1)S(1)} %copy.80), channel_id=1, replica_groups=mesh['freq'=32,'rcv'=8] {'freq'}, dimensions={0} | all-to-all | bytes 393216 | tf_op jit(solution)/shard_map/all_to_all | solution.py:61
  139.6 0.1 copy.81
  139.6 1.5 fusion.10
  141.1 0.3 fusion.13
  141.4 0.2 copy.83
  141.6 13.9 %all_to_all.115 = bf16[3,2,128,128]{3,1,0,2:T(2,128)(2,1)S(1)} all-to-all(bf16[3,2,128,128]{3,1,0,2:T(2,128)(2,1)S(1)} %copy.83), channel_id=1, replica_groups=mesh['freq'=32,'rcv'=8] {'freq'}, dimensions={2} | all-to-all | bytes 393216 | tf_op jit(solution)/shard_map/all_to_all | solution.py:38
  155.6 0.1 copy.84
  155.7 0.1 fusion.78
  155.8 0.4 fusion.22
  156.2 0.2 copy-done.5
  156.4 0.4 fusion.20
  156.8 1.3 fusion.4
  158.1 1.5 copy.87
  159.6 2.2 %fusion.5 = bf16[768,4,128]{0,2,1:T(8,128)(2,1)} fusion(f32[4,128,768]{2,1,0:T(8,128)S(1)} %fusion.20, bf16[2,4,96,768]{3,2,1,0:T(8,128)(2,1)S(1)} %copy-done, bf16[96,1,4,128]{3,2,1,0:T(4,128)(2,1)} %copy-done.5), kind=kOutput, calls=%fused_computation.15 | convolution fusion | flops 76283904 | bytes 3047424 | tf_op jit(solution)/shard_map/key,ekn->ykn/dot_general | solution.py:46
  161.8 1.5 copy.88
  163.3 0.1 pad_maximum_fusion.2
  163.5 0.2 copy.89
  163.6 24.9 %all_to_all.116 = bf16[8,96,2,4,128]{4,1,3,2,0:T(8,128)(2,1)S(1)} all-to-all(bf16[8,96,2,4,128]{4,1,3,2,0:T(8,128)(2,1)S(1)} %copy.89), channel_id=1, replica_groups=mesh['freq'=32,'rcv'=8] {'rcv'}, dimensions={0} | all-to-all | bytes 3145728 | tf_op jit(solution)/shard_map/all_to_all | solution.py:16
  188.6 0.2 convert_reduce_fusion
  188.8 0.7 copy-done.4
  189.5 0.2 fusion.67
  189.8 0.2 fusion.68
  190.0 0.2 convolution_subtract_fusion
  190.3 0.2 convolution_add_fusion
  190.6 11.3 %all_to_all.117 = bf16[8,2,4,16,128]{4,3,2,1,0:T(8,128)(2,1)S(1)} all-to-all(bf16[8,2,4,16,128]{4,3,2,1,0:T(8,128)(2,1)S(1)} %fusion.44), channel_id=1, replica_groups=mesh['freq'=32,'rcv'=8] {'rcv'}, dimensions={0} | all-to-all | bytes 524288 | tf_op jit(solution)/shard_map/all_to_all | solution.py:16
  201.9 0.7 convert_reduce_fusion.1
  (22 shorter events, 0.2 us)
Async XLA Ops:
  0.6 23.3 %copy-start = (bf16[2,4,96,768]{3,2,1,0:T(8,128)(2,1)S(1)}, bf16[2,4,96,768]{3,2,1,0:T(8,128)(2,1)}, u32[]{:S(2)}) copy-start(bf16[2,4,96,768]{3,2,1,0:T(8,128)(2,1)} %param.3) | copy-start | bytes 3538948
  29.7 1.6 copy-start.1
  59.6 16.8 %copy-start.10 = (s32[3,128]{1,0:T(4,128)S(1)}, s32[3,128]{1,0:T(4,128)}, u32[]{:S(2)}) copy-start(s32[3,128]{1,0:T(4,128)} %param.5) | copy-start | bytes 4612
  60.6 15.8 %all-to-all-start.2 = ((bf16[96,2,4,128]{3,2,1,0:T(4,128)(2,1)}), bf16[96,2,4,128]{3,2,1,0:T(4,128)(2,1)S(1)}, u32[]{:S(2)}, u32[]{:S(2)}) async-start(bf16[96,2,4,128]{3,2,1,0:T(4,128)(2,1)} %copy.69), calls=%async_computation.2 | async-start | bytes 393216 | tf_op jit(solution)/shard_map/all_to_all | solution.py:61
  66.7 10.6 %copy-start.8 = (f32[1,128,512]{2,1,0:T(8,128)}, f32[1,128,512]{2,1,0:T(8,128)S(1)}, u32[]{:S(2)}) copy-start(f32[1,128,512]{2,1,0:T(8,128)S(1)} %get-tuple-element.9) | copy-start | bytes 786436
  66.7 10.6 %copy-start.9 = (f32[1,128,512]{2,1,0:T(8,128)}, f32[1,128,512]{2,1,0:T(8,128)S(1)}, u32[]{:S(2)}) copy-start(f32[1,128,512]{2,1,0:T(8,128)S(1)} %get-tuple-element.10) | copy-start | bytes 786436
  76.8 14.7 %copy-start.6 = (bf16[3,128,512]{2,1,0:T(8,128)(2,1)}, bf16[3,128,512]{2,1,0:T(8,128)(2,1)S(1)}, u32[]{:S(2)}) copy-start(bf16[3,128,512]{2,1,0:T(8,128)(2,1)S(1)} %fusion.7) | copy-start | bytes 1179652
  91.4 0.7 copy-start.3
  97.8 1.6 copy-start.2
  141.1 15.1 %copy-start.7 = (bf16[3,128,512]{2,1,0:T(8,128)(2,1)}, bf16[3,128,512]{2,1,0:T(8,128)(2,1)S(1)}, u32[]{:S(2)}) copy-start(bf16[3,128,512]{2,1,0:T(8,128)(2,1)S(1)} %fusion.10) | copy-start | bytes 1179652
  155.7 0.6 copy-start.5
  188.6 0.9 copy-start.4
where the time goes:
time: 203 us
  blocking collectives  152 us (75%)
  matrix products  15.8 us (8%)
  local copies, waits for them, and re-layouts  14.8 us (7%)
  waiting for transfers between devices  9.65 us (5%)
  starting transfers between devices  5.02 us (2%)
  other arithmetic  3.97 us (2%)
    all_to_all x4, blocking collectives, sum_at_owner(): lax.all_to_all(parts, axis, split_axis=0, concat_axis=0, tiled=True)  89.2 us
    all_to_all x3, blocking collectives, fourier_spectrum(): lax.all_to_all(local_spectra, 'freq', split_axis=2, concat_axis=0, tiled=...  48.4 us
    all_to_all x1, blocking collectives, to_time(): lax.all_to_all(summed.astype(jnp.bfloat16), 'freq', split_axis=0, concat_...  14.6 us
    dot_general x12, matrix products, product(): jnp.einsum('key,ekn->ykn', left_operand, right_operand, preferred_element...  11.2 us
    all_to_all x1, waiting for transfers between devices, to_time(): lax.all_to_all(summed.astype(jnp.bfloat16), 'freq', split_axis=0, concat_...  9.65 us
    add x3, local copies, waits for them, and re-layouts, make_term(): product(reflection[0], spec_imag)  5.38 us
    sub x3, local copies, waits for them, and re-layouts, make_term(): product(reflection[0], spectrum_real_rows)  5.38 us
    all_to_all x1, starting transfers between devices, to_time(): lax.all_to_all(summed.astype(jnp.bfloat16), 'freq', split_axis=0, concat_...  5.02 us
  transfers between devices with their start and end apart: 1, of which 1 were waited for; matrix products, arithmetic and copies ran while one was open for 1% of the time, Pallas kernels for 0%

commit v1 on v0

v1 whole, which is shorter than its diff:
```python
import functools
import math

import jax
import jax.numpy as jnp
import ml_dtypes
import numpy as np
from jax import lax
from jax.experimental import pallas as pl
from jax.experimental.pallas import tpu as pltpu
from jax.sharding import Mesh
from jax.sharding import PartitionSpec as P

F32 = jnp.float32
BF16 = jnp.bfloat16
RCV = ("xh", "y")
OWNERS = ("xh", "y", "freq")
TRACES = ("y", "freq")


def fourier_table(samples, bins_of_owner):
    phase = (bins_of_owner[:, None] * np.arange(samples)[None, :]) % samples
    angle = 2.0 * math.pi / samples * phase
    rows = np.concatenate([np.cos(angle), -np.sin(angle)], axis=0) / math.sqrt(samples)
    return rows.astype(np.float32).astype(ml_dtypes.bfloat16)


def dot(a, b, da, db):
    return lax.dot_general(a, b, (((da,), (db,)), ((), ())), preferred_element_type=F32)


def run(kernel, out, scratch, *args):
    return pl.pallas_call(
        kernel,
        out_shape=out,
        in_specs=[pl.BlockSpec(memory_space=pltpu.VMEM)] * len(args),
        out_specs=jax.tree.map(lambda _: pl.BlockSpec(memory_space=pltpu.VMEM), out),
        scratch_shapes=scratch,
        compiler_params=pltpu.CompilerParams(vmem_limit_bytes=32 * 2**20),
    )(*args)


def put_spectrum(field, table, rows_ref, i, step, conj):
    n = table.shape[0] // 2
    v = dot(table, field, 1, 1)
    rows_ref[pl.ds(2 * i, n, stride=step), :] = v[:n]
    im = v[n:]
    rows_ref[pl.ds(2 * i + 1, n, stride=step), :] = -im if conj else im


def flush(rows_ref, send_ref):
    rows = rows_ref[...].astype(BF16)
    for h in range(send_ref.shape[0]):
        send_ref[h] = rows


def first_kernel(direct_ref, table_ref, send_ref, out_rows):
    n = direct_ref.shape[0]
    for i in range(n):
        put_spectrum(direct_ref[i], table_ref[...], out_rows, i, 2 * n, False)
    flush(out_rows, send_ref)


def trace_kernel(n, conj_in, conj_out, add, *refs):
    if add:
        got_ref, onset_ref, table_ref, direct_ref, field_ref, send_ref, in_rows, out_rows = refs
    else:
        got_ref, onset_ref, table_ref, field_ref, send_ref, in_rows, out_rows = refs
    table = table_ref[...]
    bins = table.shape[0] // 2
    step = 2 * n
    in_rows[...] = got_ref[...].astype(F32)
    for i in range(n):
        re = in_rows[pl.ds(2 * i, bins, stride=step), :]
        im = in_rows[pl.ds(2 * i + 1, bins, stride=step), :]
        both = jnp.concatenate([re, -im if conj_in else im], axis=0).astype(BF16)
        trace = dot(both, table, 0, 0) * 2.0
        sample = lax.broadcasted_iota(jnp.int32, trace.shape, 1)
        trace = jnp.where(sample < onset_ref[:, i : i + 1], trace, 0.0)
        if add:
            trace = direct_ref[i].astype(F32) + trace
        field = trace.astype(BF16)
        field_ref[i] = field
        put_spectrum(field, table, out_rows, i, step, conj_out)
    flush(out_rows, send_ref)


def weave_kernel(got_ref, w_ref, even_odd):
    peers, _, block, half = got_ref.shape
    lanes = even_odd.shape[1]
    for col in range(0, half, lanes):
        for out, parts in ((0, (0, 1)), (1, (1, 0))):
            for b in range(peers):
                first, second = (got_ref[b, c, :, col : col + lanes].astype(F32) for c in parts)
                start = 2 * b * block
                even_odd[pl.ds(start, block, stride=2), :] = first
                even_odd[pl.ds(start + 1, block, stride=2), :] = second if out else -second
            at = out * half + col
            w_ref[:, at : at + lanes] = even_odd[...].astype(BF16)


def product(v_ref, w_ref):
    return dot(v_ref[...], w_ref[...], 0, 0).T


def apply_kernel(v_ref, w_ref, send_ref, rows):
    p = product(v_ref, w_ref)
    half = p.shape[0] // 2
    rows[pl.ds(0, half, stride=2), :] = p[:half]
    rows[pl.ds(1, half, stride=2), :] = p[half:]
    send_ref[...] = rows[...].astype(BF16)


def green_kernel(scale, v_ref, w_ref, minus_ref, corr_ref, rows):
    rows[...] = minus_ref[...].astype(F32)
    p = product(v_ref, w_ref)
    half = p.shape[0] // 2
    re = (p[:half] - rows[pl.ds(0, half, stride=2), :]).astype(BF16)
    im = (p[half:] + rows[pl.ds(1, half, stride=2), :]).astype(BF16)
    cross = dot(re, im, 0, 0)
    corr_ref[0] = ((dot(re, re, 0, 0) + dot(im, im, 0, 0)) * scale).astype(BF16)
    corr_ref[1] = ((cross - cross.T) * scale).astype(BF16)


def exchange(value, axes):
    return lax.all_to_all(value, axes, split_axis=0, concat_axis=0, tiled=True)


def on_device(reflection, direct, onset):
    n, focal, samples = direct.shape
    per_group = reflection.shape[1]
    block, receivers = reflection.shape[2:]
    halves, ys = lax.axis_size("xh"), lax.axis_size("y")
    groups = lax.axis_size("freq")
    bins = per_group * groups
    half = receivers // halves
    shape = jax.ShapeDtypeStruct

    order = (np.arange(groups)[None, :] * per_group + np.arange(ys)[:, None]).reshape(-1)
    table = jnp.asarray(fourier_table(samples, order))
    onset_cols = onset.T

    packed = reflection.reshape(2, per_group, block, halves, half).transpose(3, 1, 0, 2, 4)
    got = exchange(packed.reshape(halves * ys, 2, block, half), RCV)
    w = run(
        weave_kernel,
        shape((2 * receivers, 2 * half), BF16),
        [pltpu.VMEM((2 * receivers, focal), F32)],
        got,
    )

    rows_out = 2 * n * bins
    send_shape = shape((halves, rows_out, focal), BF16)
    field_shape = shape(direct.shape, BF16)
    rows = pltpu.VMEM((rows_out, focal), F32)

    def to_owners(send):
        parts = send.reshape(halves * bins, n, 2, focal)
        return exchange(parts, OWNERS).reshape(2 * receivers, focal)

    def to_traces(send):
        return exchange(send.reshape(bins, n, 2, focal), TRACES).reshape(rows_out, focal)

    def apply(v):
        return run(apply_kernel, shape((2 * half, focal), BF16), [pltpu.VMEM((2 * half, focal), F32)], v, w)

    plus = to_owners(run(first_kernel, send_shape, [rows], direct, table))
    summed = to_traces(apply(plus))
    focus_minus, send = run(
        functools.partial(trace_kernel, n, False, True, False),
        (field_shape, send_shape),
        [rows, rows],
        summed,
        onset_cols,
        table,
    )
    minus = to_owners(send)
    summed = to_traces(apply(minus))
    focus_plus, send = run(
        functools.partial(trace_kernel, n, True, False, True),
        (field_shape, send_shape),
        [rows, rows],
        summed,
        onset_cols,
        table,
        direct,
    )
    plus = to_owners(send)
    mine = lax.dynamic_index_in_dim(
        minus.reshape(halves, 2 * half, focal), lax.axis_index("xh"), 0, keepdims=False
    )
    partial = run(
        functools.partial(green_kernel, 1.0 / receivers),
        shape((2, focal, focal), BF16),
        [pltpu.VMEM((2 * half, focal), F32)],
        plus,
        w,
        mine,
    )
    rows_each = focal // (halves * ys)
    parts = partial.reshape(2, halves * ys, rows_each, focal).transpose(1, 0, 2, 3)
    arrived = exchange(parts, RCV).astype(F32)
    summed = arrived.reshape(halves, ys, 2, rows_each, focal).sum(axis=0)
    return focus_plus, focus_minus, summed.transpose(1, 0, 2, 3)


def solution(mesh):
    groups, rcv = mesh.shape["freq"], mesh.shape["rcv"]
    fine = Mesh(mesh.devices.reshape(groups, 2, rcv // 2), ("freq", "xh", "y"))
    traces = ("xh", "y", "freq")
    return jax.shard_map(
        on_device,
        mesh=fine,
        in_specs=(P(None, "freq", RCV, None), P(traces, None, None), P(traces, None)),
        out_specs=(P(traces, None, None), P(traces, None, None), P(None, "freq", RCV, None)),
        check_vma=False,
    )
```

time: 203 us -> 162 us (0.80)
  blocking collectives: 152 us -> 52.5 us
  waiting for transfers between devices: 9.65 us -> 62.1 us
  starting transfers between devices: 5.02 us -> 32.8 us
  matrix products: 15.8 us -> 0 us
  local copies, waits for them, and re-layouts: 14.8 us -> 4.79 us
  Pallas kernels: 0 us -> 8.62 us
  other arithmetic: 3.97 us -> 0.01 us
    all_to_all x8 -> x3, blocking collectives: 152 us -> 52.5 us  [exchange(): return lax.all_to_all(value, axes, split_axis=0, concat_axis=0, tiled=True)]
    all_to_all x1 -> x4, waiting for transfers between devices: 9.65 us -> 62.1 us  [exchange(): return lax.all_to_all(value, axes, split_axis=0, concat_axis=0, tiled=True)]
    all_to_all x1 -> x4, starting transfers between devices: 5.02 us -> 32.8 us  [exchange(): return lax.all_to_all(value, axes, split_axis=0, concat_axis=0, tiled=True)]
    dot_general x21 -> x0, matrix products: 15.8 us -> none  [the longest x12 11.2 us: product(): jnp.einsum('key,ekn->ykn', left_operand, right_operand, preferred_element...]
    pallas_call x0 -> x7, Pallas kernels: none -> 8.62 us  [run(): pl.pallas_call(kernel, out_shape=out, in_specs=[pl.BlockSpec(memory_space...]
    add x3 -> x0, local copies, waits for them, and re-layouts: 5.38 us -> none  [make_term(): product(reflection[0], spec_imag)]
    sub x3 -> x0, local copies, waits for them, and re-layouts: 5.38 us -> none  [make_term(): product(reflection[0], spectrum_real_rows)]
    reshape x0 -> x3, local copies, waits for them, and re-layouts: none -> 4 us  [the longest x2 3.99 us: on_device(): reflection.reshape(2, per_group, block, halves, half)]
  transfers between devices with their start and end apart: 1 -> 4, of which waited for: 1 -> 4; matrix products, arithmetic and copies ran while one was open for 1% -> 0% of each run, Pallas kernels for 0% -> 1%
where the time goes in v1:
time: 162 us
  waiting for transfers between devices  62.1 us (38%)
  blocking collectives  52.5 us (32%)
  starting transfers between devices  32.8 us (20%)
  Pallas kernels  8.62 us (5%)
  local copies, waits for them, and re-layouts  4.79 us (3%)
    all_to_all x4, waiting for transfers between devices, exchange(): return lax.all_to_all(value, axes, split_axis=0, concat_axis=0, tiled=True)  62.1 us
    all_to_all x3, blocking collectives, exchange(): return lax.all_to_all(value, axes, split_axis=0, concat_axis=0, tiled=True)  52.5 us
    all_to_all x4, starting transfers between devices, exchange(): return lax.all_to_all(value, axes, split_axis=0, concat_axis=0, tiled=True)  32.8 us
    pallas_call x7, Pallas kernels, run(): pl.pallas_call(kernel, out_shape=out, in_specs=[pl.BlockSpec(memory_space...  8.62 us
    reshape x2, local copies, waits for them, and re-layouts, on_device(): reflection.reshape(2, per_group, block, halves, half)  3.99 us
  transfers between devices with their start and end apart: 4, of which 4 were waited for; matrix products, arithmetic and copies ran while one was open for 0% of the time, Pallas kernels for 1%

profile of v1, /device:TPU:2, one launch (start us, length us, event | category | flops | bytes accessed | tf_op | source)
XLA Modules:
  0.0 161.6 jit_solution(9160921273515004637)
XLA Ops:
  0.6 2.8 %reshape.53 = bf16[2,4,96,2,384]{4,3,2,1,0:T(2,128)(2,1)S(1)} reshape(bf16[2,4,96,768]{3,2,1,0:T(8,128)(2,1)} %param.4) | data formatting | bytes 2359296 | tf_op jit(solution)/shard_map/reshape | solution.py:143
  3.4 1.2 copy.12
  4.6 0.0 copy-start
  4.6 0.0 copy-start.2
  4.6 6.2 %all-to-all-start.1 = ((bf16[8,2,96,384]{3,2,1,0:T(8,128)(2,1)}), bf16[8,2,96,384]{3,2,1,0:T(8,128)(2,1)S(1)}, u32[]{:S(2)}, u32[]{:S(2)}) async-start(bf16[8,2,96,384]{3,2,1,0:T(8,128)(2,1)} %bitcast.3), calls=%async_computation.1 | async-start | bytes 2359296 | tf_op jit(solution)/shard_map/all_to_all | solution.py:126
  10.8 0.0 copy-done
  10.8 0.0 copy-done.2
  10.8 1.1 shard_map.67
  12.0 15.7 %all-to-all-done.1.got_ref = bf16[8,2,96,384]{3,2,1,0:T(8,128)(2,1)S(1)} async-done(((bf16[8,2,96,384]{3,2,1,0:T(8,128)(2,1)}), bf16[8,2,96,384]{3,2,1,0:T(8,128)(2,1)S(1)}, u32[]{:S(2)}, u32[]{:S(2)}) %all-to-all-start.1) | async-done | bytes 1179680 | tf_op jit(solution)/shard_map/all_to_all | solution.py:126
  27.7 14.0 %all-to-all-start = ((bf16[256,3,2,128]{3,2,1,0:T(2,128)(2,1)}), bf16[256,3,2,128]{3,2,1,0:T(2,128)(2,1)}, u32[]{:S(2)}, u32[]{:S(2)}) async-start(bf16[256,3,2,128]{3,2,1,0:T(2,128)(2,1)} %bitcast), calls=%async_computation | async-start | bytes 786432 | tf_op jit(solution)/shard_map/all_to_all | solution.py:126
  41.7 0.6 shard_map.68.w_ref
  42.3 16.2 %all-to-all-done = bf16[256,3,2,128]{3,2,1,0:T(2,128)(2,1)} async-done(((bf16[256,3,2,128]{3,2,1,0:T(2,128)(2,1)}), bf16[256,3,2,128]{3,2,1,0:T(2,128)(2,1)}, u32[]{:S(2)}, u32[]{:S(2)}) %all-to-all-start) | async-done | bytes 393248 | tf_op jit(solution)/shard_map/all_to_all | solution.py:126
  58.5 0.0 copy-start.4
  58.5 0.0 copy-start.1
  58.5 2.4 %shard_map.69 = bf16[768,128]{1,0:T(8,128)(2,1)} custom-call(bf16[1536,128]{1,0:T(8,128)(2,1)} %bitcast.1.v_ref, bf16[1536,768]{1,0:T(8,128)(2,1)S(1)} %shard_map.68.w_ref), custom_call_target="tpu_custom_call" | custom-call | tf_op jit(solution)/shard_map/pallas_call | solution.py:33
  60.9 6.7 %all-to-all-start.2 = ((bf16[128,3,2,128]{3,2,1,0:T(2,128)(2,1)}), bf16[128,3,2,128]{3,2,1,0:T(2,128)(2,1)S(1)}, u32[]{:S(2)}, u32[]{:S(2)}) async-start(bf16[128,3,2,128]{3,2,1,0:T(2,128)(2,1)} %bitcast.4), calls=%async_computation.2 | async-start | bytes 393216 | tf_op jit(solution)/shard_map/all_to_all | solution.py:126
  67.6 0.0 copy-done.4
  67.6 0.1 copy.13
  67.7 12.4 %all-to-all-done.2 = bf16[128,3,2,128]{3,2,1,0:T(2,128)(2,1)S(1)} async-done(((bf16[128,3,2,128]{3,2,1,0:T(2,128)(2,1)}), bf16[128,3,2,128]{3,2,1,0:T(2,128)(2,1)S(1)}, u32[]{:S(2)}, u32[]{:S(2)}) %all-to-all-start.2) | async-done | bytes 196640 | tf_op jit(solution)/shard_map/all_to_all | solution.py:126
  80.1 0.0 copy-done.1
  80.2 1.3 shard_map.70
  81.4 23.4 %all_to_all.35 = bf16[256,3,2,128]{3,2,1,0:T(2,128)(2,1)S(1)} all-to-all(bf16[256,3,2,128]{3,2,1,0:T(2,128)(2,1)S(1)} %bitcast.34), channel_id=1, replica_groups=mesh['freq'=32,'xh'=2,'y'=4] {'xh','y','freq'}, dimensions={0} | all-to-all | bytes 786432 | tf_op jit(solution)/shard_map/all_to_all | solution.py:126
  104.9 0.0 copy-start.3
  104.9 0.6 shard_map.71
  105.6 18.6 %all_to_all.36 = bf16[128,3,2,128]{3,2,1,0:T(2,128)(2,1)S(1)} all-to-all(bf16[128,3,2,128]{3,2,1,0:T(2,128)(2,1)S(1)} %bitcast.30), channel_id=1, replica_groups=mesh['freq'=32,'xh'=2,'y'=4] {'y','freq'}, dimensions={0} | all-to-all | bytes 393216 | tf_op jit(solution)/shard_map/all_to_all | solution.py:126
  124.1 0.0 copy-done.3
  124.1 1.6 shard_map.72
  125.7 6.0 %all-to-all-start.5 = ((bf16[256,3,2,128]{3,2,1,0:T(2,128)(2,1)}), bf16[256,3,2,128]{3,2,1,0:T(2,128)(2,1)S(1)}, u32[]{:S(2)}, u32[]{:S(2)}) async-start(bf16[256,3,2,128]{3,2,1,0:T(2,128)(2,1)} %bitcast.11), calls=%async_computation.5 | async-start | bytes 786432 | tf_op jit(solution)/shard_map/all_to_all | solution.py:126
  131.7 17.7 %all-to-all-done.5 = bf16[256,3,2,128]{3,2,1,0:T(2,128)(2,1)S(1)} async-done(((bf16[256,3,2,128]{3,2,1,0:T(2,128)(2,1)}), bf16[256,3,2,128]{3,2,1,0:T(2,128)(2,1)S(1)}, u32[]{:S(2)}, u32[]{:S(2)}) %all-to-all-start.5) | async-done | bytes 393248 | tf_op jit(solution)/shard_map/all_to_all | solution.py:126
  149.5 0.9 shard_map.73
  150.5 10.5 %all_to_all.37 = bf16[8,2,16,128]{3,2,1,0:T(8,128)(2,1)S(1)} all-to-all(bf16[8,2,16,128]{3,2,1,0:T(8,128)(2,1)S(1)} %bitcast.36), channel_id=1, replica_groups=mesh['freq'=32,'xh'=2,'y'=4] {'xh','y'}, dimensions={0} | all-to-all | bytes 131072 | tf_op jit(solution)/shard_map/all_to_all | solution.py:126
  161.0 0.6 copy.15
  (3 shorter events, 0.0 us)
Async XLA Ops:
  4.6 6.2 %copy-start = (bf16[256,512]{1,0:T(8,128)(2,1)S(1)}, bf16[256,512]{1,0:T(8,128)(2,1)}, u32[]{:S(2)}) copy-start(bf16[256,512]{1,0:T(8,128)(2,1)} %constant.16.clone.table_ref.refs_2_) | copy-start | bytes 786436
  4.6 6.2 %copy-start.2 = (bf16[3,128,512]{2,1,0:T(8,128)(2,1)S(1)}, bf16[3,128,512]{2,1,0:T(8,128)(2,1)}, u32[]{:S(2)}) copy-start(bf16[3,128,512]{2,1,0:T(8,128)(2,1)} %refs_3_.1) | copy-start | bytes 1179652
  4.6 23.1 %all-to-all-start.1 = ((bf16[8,2,96,384]{3,2,1,0:T(8,128)(2,1)}), bf16[8,2,96,384]{3,2,1,0:T(8,128)(2,1)S(1)}, u32[]{:S(2)}, u32[]{:S(2)}) async-start(bf16[8,2,96,384]{3,2,1,0:T(8,128)(2,1)} %bitcast.3), calls=%async_computation.1 | async-start | bytes 2359296 | tf_op jit(solution)/shard_map/all_to_all | solution.py:126
  27.7 30.8 %all-to-all-start = ((bf16[256,3,2,128]{3,2,1,0:T(2,128)(2,1)}), bf16[256,3,2,128]{3,2,1,0:T(2,128)(2,1)}, u32[]{:S(2)}, u32[]{:S(2)}) async-start(bf16[256,3,2,128]{3,2,1,0:T(2,128)(2,1)} %bitcast), calls=%async_computation | async-start | bytes 786432 | tf_op jit(solution)/shard_map/all_to_all | solution.py:126
  58.5 9.1 %copy-start.4 = (s32[3,128]{1,0:T(4,128)S(1)}, s32[3,128]{1,0:T(4,128)}, u32[]{:S(2)}) copy-start(s32[3,128]{1,0:T(4,128)} %param.6) | copy-start | bytes 4612
  58.5 21.6 %copy-start.1 = (bf16[256,512]{1,0:T(8,128)(2,1)S(1)}, bf16[256,512]{1,0:T(8,128)(2,1)}, u32[]{:S(2)}) copy-start(bf16[256,512]{1,0:T(8,128)(2,1)} %constant.16.clone.table_ref.refs_2_) | copy-start | bytes 786436
  60.9 19.2 %all-to-all-start.2 = ((bf16[128,3,2,128]{3,2,1,0:T(2,128)(2,1)}), bf16[128,3,2,128]{3,2,1,0:T(2,128)(2,1)S(1)}, u32[]{:S(2)}, u32[]{:S(2)}) async-start(bf16[128,3,2,128]{3,2,1,0:T(2,128)(2,1)} %bitcast.4), calls=%async_computation.2 | async-start | bytes 393216 | tf_op jit(solution)/shard_map/all_to_all | solution.py:126
  104.9 19.2 %copy-start.3 = (bf16[3,128,512]{2,1,0:T(8,128)(2,1)S(1)}, bf16[3,128,512]{2,1,0:T(8,128)(2,1)}, u32[]{:S(2)}) copy-start(bf16[3,128,512]{2,1,0:T(8,128)(2,1)} %refs_3_.1) | copy-start | bytes 1179652
  125.7 23.8 %all-to-all-start.5 = ((bf16[256,3,2,128]{3,2,1,0:T(2,128)(2,1)}), bf16[256,3,2,128]{3,2,1,0:T(2,128)(2,1)S(1)}, u32[]{:S(2)}, u32[]{:S(2)}) async-start(bf16[256,3,2,128]{3,2,1,0:T(2,128)(2,1)} %bitcast.11), calls=%async_computation.5 | async-start | bytes 786432 | tf_op jit(solution)/shard_map/all_to_all | solution.py:126
